TPU v7x, 32 devices: a whole 2x2x4 slice. The times are simulated.
32 devices in a mesh: clip: 2 (over y), seq: 4 (over z), head: 4 (over x, core).
Axes of the slice: x: 2, y: 2, z: 4, core: 2. Of those that a mesh axis runs over, the one named last changes fastest.
Arguments:
- queries: bfloat16 [16, 4, 16, 3072], P(('clip', 'head'), 'seq'), parts along dimension 0, may hold values from -15 to 15
- attn_keys: bfloat16 [16, 4, 16, 3072], P(('clip', 'head'), 'seq'), parts along dimension 0, may hold values from -5 to 5
- attn_values: bfloat16 [16, 4, 16, 3072], P(('clip', 'head'), 'seq'), parts along dimension 0, may hold values from -5 to 5
- residual: bfloat16 [16, 4, 16, 5120], P(('clip', 'head'), 'seq'), parts along dimension 0, may hold values from -6 to 6
- out_weight: bfloat16 [3072, 5120], P('head', 'seq'), may hold values from -0.109375 to 0.109375
- out_gate: float32 [5120], replicated, may hold values from 0.3 to 3
- head_shift: float32 [5120], replicated, may hold values from -3 to 3
- head_scale: float32 [5120], replicated, may hold values from -1.5 to 1.5
- head_weight: bfloat16 [5120, 64], replicated, may hold values from -0.078125 to 0.078125
- head_bias: float32 [64], replicated, may hold values from -3 to 3
- conv_weight: bfloat16 [3, 3, 3, 16, 384], replicated, may hold values from -0.3125 to 0.3125
- conv_bias: float32 [384], replicated, may hold values from -3 to 3
- norm_gain: float32 [384], replicated, may hold values from 0.5 to 2
Outputs:
- hidden: bfloat16 [16, 4, 16, 5120], P(('clip', 'head'), 'seq'), parts along dimension 0
- features: bfloat16 [16, 8, 32, 384], P(('clip', 'head'), 'seq'), parts along dimension 0
There are 2 independent parts, one for each index of `clip`. A program takes and returns all parts, laid end to end along the dimension named above; an argument that names none is the same for every part. Nothing has to cross between parts.
All inputs are finite; a program needn't handle non-finite values.
Results may differ from a plain program's by a relative error of at most 0.013.
Values may be sent and summed in bfloat16 or wider, within the bound.
No kernel may reach another device: no remote copies, remote signals or barrier semaphores. Data moves between devices by JAX's collectives and lax.ppermute only.
A program may use at most 128 MiB of HBM per device.

v0:
```python
import jax
import jax.numpy as jnp
from jax import lax
from jax.sharding import PartitionSpec as P

HEAD_DIM = 128


def from_behind(value, axis, steps):
    count = lax.axis_size(axis)
    first, last = (max(0, -steps), min(count, count - steps))
    return lax.ppermute(value, axis, [(source, source + steps) for source in range(first, last)])


def padded_2(x, sides, width):
    for axis, dim in sides:
        peers, length = (lax.axis_size(axis), x.shape[dim])
        up = [(i, (i + 1) % peers) for i in range(peers - 1)]
        down = [(j, i) for i, j in up]
        last = lax.slice_in_dim(x, length - width, length, axis=dim)
        first = lax.slice_in_dim(x, 0, width, axis=dim)
        before = lax.ppermute(last, axis, up)
        after = lax.ppermute(first, axis, down)
        x = jnp.concatenate([before, x, after], axis=dim)
    return x


def head_latent(hidden, head_shift, head_scale, head_weight, head_bias):
    values = hidden.astype(jnp.float32)
    center = values - jnp.mean(values, -1, keepdims=True)
    spread = jnp.mean(center * center, -1, keepdims=True)
    normed = (center * lax.rsqrt(spread + 1e-06) * (1.0 + head_scale) + head_shift).astype(
        jnp.bfloat16
    )
    flat = normed.reshape(-1, normed.shape[-1])
    latent = (jnp.dot(flat, head_weight, preferred_element_type=jnp.float32) + head_bias).astype(
        jnp.bfloat16
    )
    frames, height, breadth = (hidden.shape[0], hidden.shape[1], hidden.shape[2])
    channels = head_weight.shape[1] // 4
    patches = latent.reshape(frames, height, breadth, 2, 2, channels).transpose(0, 1, 3, 2, 4, 5)
    return patches.reshape(frames, height * 2, breadth * 2, channels)


def convolve(padded, frames, conv_weight, conv_bias, norm_gain):
    height = padded.shape[1] - 2
    breadth = padded.shape[2] - 2
    stacked = jnp.concatenate(
        [
            padded[
                time_off : time_off + frames,
                row_off : row_off + height,
                col_off : col_off + breadth,
            ]
            for time_off in range(3)
            for row_off in range(3)
            for col_off in range(3)
        ],
        -1,
    )
    kernel = conv_weight.reshape(-1, conv_weight.shape[-1])
    linear = (
        jnp.dot(stacked.reshape(-1, stacked.shape[-1]), kernel, preferred_element_type=jnp.float32)
        + conv_bias
    )
    normed = linear * lax.rsqrt(jnp.mean(linear * linear, -1, keepdims=True) + 1e-06) * norm_gain
    return jax.nn.silu(normed).astype(jnp.bfloat16).reshape(frames, height, breadth, -1)


def attend_block(carried, block_keys, block_values, query_heads):
    running, denominator, weighted = carried
    scores = jnp.einsum("hqd,khd->hqk", query_heads, block_keys, preferred_element_type=jnp.float32)
    scores = scores * query_heads.shape[-1] ** (-0.5)
    newmax = jnp.maximum(running, jnp.max(scores, -1))
    factor = jnp.exp(running - newmax)
    weights = jnp.exp(scores - newmax[..., None])
    denominator = denominator * factor + jnp.sum(weights, -1)
    product = jnp.einsum(
        "hqk,khd->hqd",
        weights.astype(jnp.bfloat16),
        block_values,
        preferred_element_type=jnp.float32,
    )
    weighted = weighted * factor[..., None] + product
    return (newmax, denominator, weighted)


def fold_pieces(query_heads, carried, pieces):
    key_piece, value_piece = pieces
    frames, height, breadth = (key_piece.shape[0], key_piece.shape[1], key_piece.shape[2])
    heads_here, head_width = (query_heads.shape[0], query_heads.shape[2])
    group_rows = 4

    def regroup(one_piece):
        shaped = one_piece.reshape(
            frames, height // group_rows, group_rows, breadth, heads_here, head_width
        )
        shaped = shaped.transpose(1, 0, 2, 3, 4, 5)
        return shaped.reshape(
            height // group_rows, frames * group_rows * breadth, heads_here, head_width
        )

    def advance(inner, blocks):
        return (attend_block(inner, blocks[0], blocks[1], query_heads), None)

    carried, _ = lax.scan(advance, carried, (regroup(key_piece), regroup(value_piece)))
    return carried


def on_device(
    queries,
    attn_keys,
    attn_values,
    residual,
    out_weight,
    out_gate,
    head_shift,
    head_scale,
    head_weight,
    head_bias,
    conv_weight,
    conv_bias,
    norm_gain,
):
    head_count = lax.axis_size("head")
    frames_dev = queries.shape[0]
    group_width = queries.shape[3] // head_count
    head_width = HEAD_DIM
    heads_here = group_width // head_width
    local_queries, local_keys, local_values = (
        lax.all_to_all(queries, "head", split_axis=3, concat_axis=0, tiled=True),
        lax.all_to_all(attn_keys, "head", split_axis=3, concat_axis=0, tiled=True),
        lax.all_to_all(attn_values, "head", split_axis=3, concat_axis=0, tiled=True),
    )
    frames_all, height, breadth = (
        local_queries.shape[0],
        local_queries.shape[1],
        local_queries.shape[2],
    )
    count = frames_all * height * breadth
    query_heads = local_queries.reshape(count, heads_here, head_width).transpose(1, 0, 2)
    initial = (
        jnp.full((heads_here, count), -1e30, jnp.float32),
        jnp.zeros((heads_here, count), jnp.float32),
        jnp.zeros((heads_here, count, head_width), jnp.float32),
    )
    carried = fold_pieces(
        query_heads,
        initial,
        (
            lax.all_gather(local_keys, "seq", axis=1, tiled=True),
            lax.all_gather(local_values, "seq", axis=1, tiled=True),
        ),
    )
    running, denominator, weighted = carried
    attended = (weighted / denominator[..., None]).astype(jnp.bfloat16)
    attended = attended.transpose(1, 0, 2).reshape(count, group_width)
    partial_value = jnp.dot(
        attended,
        lax.all_gather(out_weight, "seq", axis=1, tiled=True),
        preferred_element_type=jnp.float32,
    )
    partial_value = partial_value.reshape(frames_all, height, breadth, partial_value.shape[-1])
    owned = lax.psum_scatter(
        partial_value.astype(jnp.bfloat16), "head", scatter_dimension=0, tiled=True
    ).astype(jnp.float32)
    hidden = (residual.astype(jnp.float32) + out_gate * owned).astype(jnp.bfloat16)
    own_video = head_latent(hidden, head_shift, head_scale, head_weight, head_bias)
    earlier = from_behind(own_video, "head", 1)
    video = jnp.concatenate([earlier, own_video], 0)
    extended = padded_2(video, (("seq", 1),), 1)
    padded = jnp.pad(extended, ((0, 0), (0, 0), (1, 1), (0, 0)))
    features = convolve(padded, frames_dev, conv_weight, conv_bias, norm_gain)
    return (hidden, features)


def solution(mesh):
    return jax.shard_map(
        on_device,
        mesh=mesh,
        in_specs=(
            P(("clip", "head"), "seq", None, None),
            P(("clip", "head"), "seq", None, None),
            P(("clip", "head"), "seq", None, None),
            P(("clip", "head"), "seq", None, None),
            P("head", "seq"),
            P(),
            P(),
            P(),
            P(),
            P(),
            P(),
            P(),
            P(),
        ),
        out_specs=(P(("clip", "head"), "seq", None, None), P(("clip", "head"), "seq", None, None)),
        check_vma=False,
    )
```

profile of v0, /device:TPU:2, one launch (start us, length us, event | category | flops | bytes accessed | tf_op | source)
XLA Modules:
  0.0 232.1 jit_solution(3632974338613475676)
XLA Ops:
  7.2 0.0 copy-start
  7.2 0.0 all-gather.2.cloned.1.call-start
  7.2 0.7 all-gather.2.cloned.1.call-update
  7.9 0.2 copy-done.5
  8.2 1.8 copy.79
  10.0 2.3 reshape.122
  12.3 3.4 %all-to-all-start.1 = ((bf16[4,2,12288]{2,1,0:T(2,128)(2,1)}), bf16[4,2,12288]{2,1,0:T(2,128)(2,1)S(1)}, u32[]{:S(2)}, u32[]{:S(2)}) async-start(bf16[4,2,12288]{2,1,0:T(2,128)(2,1)} %reshape.122), calls=%async_computation.1 | async-start | bytes 393216 | tf_op jit(solution)/shard_map/all_to_all | solution.py:132
  15.6 1.8 copy.75
  17.5 0.0 copy-start.7
  17.5 2.3 reshape.124
  19.8 4.4 %all-to-all-start = ((bf16[4,2,12288]{2,1,0:T(2,128)(2,1)}), bf16[4,2,12288]{2,1,0:T(2,128)(2,1)S(1)}, u32[]{:S(2)}, u32[]{:S(2)}) async-start(bf16[4,2,12288]{2,1,0:T(2,128)(2,1)} %reshape.124), calls=%async_computation | async-start | bytes 393216 | tf_op jit(solution)/shard_map/all_to_all | solution.py:131
  24.2 1.8 copy.84
  26.0 2.3 reshape.126
  28.3 1.2 reshape.123
  29.4 1.1 copy.93
  30.6 0.0 all-to-all-done
  30.6 4.0 %all-to-all-start.2 = ((bf16[4,2,12288]{2,1,0:T(2,128)(2,1)}), bf16[4,2,12288]{2,1,0:T(2,128)(2,1)}, u32[]{:S(2)}, u32[]{:S(2)}) async-start(bf16[4,2,12288]{2,1,0:T(2,128)(2,1)} %reshape.126), calls=%async_computation.2 | async-start | bytes 393216 | tf_op jit(solution)/shard_map/all_to_all | solution.py:133
  34.6 0.0 reduce-scatter.2.cloned.1.call-start
  34.7 35.2 %all_gather.9 = bf16[8,4,16,768]{3,2,0,1:T(8,128)(2,1)S(1)} all-gather(bf16[8,1,16,768]{3,2,0,1:T(8,128)(2,1)S(1)} %bitcast.111), channel_id=1, replica_groups=mesh['clip'=2,'seq'=4,'head'=4] {'seq'}, dimensions={1}, use_global_device_ids=true | all-gather | bytes 983040 | tf_op jit(solution)/shard_map/all_gather | solution.py:151
  69.9 0.1 copy.82
  70.0 0.9 squeeze.9
  70.8 1.2 reshape.125
  72.0 1.1 copy.92
  73.1 0.2 reshape.115
  73.4 0.0 all-to-all-done.2
  73.4 5.6 %reshape.127 = bf16[3072,1,2,16]{3,2,1,0:T(2,128)(2,1)S(1)} reshape(bf16[4,2,12288]{2,1,0:T(2,128)(2,1)} %all-to-all-done.2) | data formatting | bytes 393216
  79.0 2.5 %copy.94 = bf16[2,1,16,4,768]{4,3,2,0,1:T(4,128)(2,1)} copy(bf16[2,1,16,4,768]{2,0,4,3,1:T(2,128)(2,1)S(1)} %bitcast.95) | data formatting | bytes 393216 | tf_op jit(solution)/shard_map/all_to_all | solution.py:133
  81.5 1.0 copy.86
  82.4 32.4 %all_gather.10 = bf16[8,4,16,768]{3,2,0,1:T(8,128)(2,1)S(1)} all-gather(bf16[8,1,16,768]{3,2,0,1:T(8,128)(2,1)S(1)} %bitcast.112), channel_id=1, replica_groups=mesh['clip'=2,'seq'=4,'head'=4] {'seq'}, dimensions={1}, use_global_device_ids=true | all-gather | bytes 983040 | tf_op jit(solution)/shard_map/all_gather | solution.py:152
  114.8 0.1 copy.87
  114.9 1.9 squeeze.10
  116.8 0.5 fusion.35
  117.3 0.5 fusion.8
  117.8 0.2 copy-done.2
  118.0 0.6 fusion.12
  118.7 0.1 copy.89
  118.8 0.2 dot_general.24
  119.1 0.0 copy-start.9
  119.1 0.0 copy-start.10
  119.1 57.9 %all-gather.2.cloned.1.call-done = bf16[768,5120]{1,0:T(8,128)(2,1)} async-done(((bf16[768,1280]{1,0:T(8,128)(2,1)}), bf16[768,5120]{1,0:T(8,128)(2,1)}) %all-gather.2.cloned.1.call-update) | async-done | bytes 7864336 | tf_op jit(solution)/shard_map/all_gather | solution.py:160
  177.0 5.6 %fusion.5 = bf16[8,1,16,5120]{3,2,0,1:T(8,128)(2,1)} fusion(bf16[8,16,768]{2,1,0:T(8,128)(2,1)S(1)} %dot_general.24, bf16[768,5120]{1,0:T(8,128)(2,1)} %all-gather.2.cloned.1.call-done), kind=kOutput, calls=%fused_computation.3 | convolution fusion | flops 1007288320 | bytes 9371648 | tf_op jit(solution)/shard_map/dot_general | solution.py:158
  182.6 0.0 reduce-scatter.2.cloned.1.call-update
  182.6 23.7 %reduce-scatter.2.cloned.1.call-done = bf16[2,1,16,5120]{3,2,0,1:T(8,128)(2,1)} async-done(((bf16[8,1,16,5120]{3,2,0,1:T(8,128)(2,1)}), bf16[2,1,16,5120]{3,2,0,1:T(8,128)(2,1)}) %reduce-scatter.2.cloned.1.call-update) | async-done | bytes 327696 | tf_op jit(solution)/shard_map/reduce_scatter | solution.py:164
  206.3 1.2 convert_reduce_fusion
  207.5 0.2 fusion.20
  207.7 0.0 copy-done.8
  207.8 0.2 fusion.23
  208.0 0.3 fusion.13
  208.3 0.1 reshape.117
  208.4 1.9 collective-permute-start
  210.4 3.3 %collective-permute-done = bf16[2,2,32,16]{3,2,1,0:T(8,128)(2,1)S(1)} collective-permute-done((bf16[2,2,32,16]{3,2,1,0:T(8,128)(2,1)S(1)}, bf16[2,2,32,16]{3,2,1,0:T(8,128)(2,1)S(1)}, u32[]{:S(2)}, u32[]{:S(2)}) %collective-permute-start) | collective-permute-done | bytes 4128 | tf_op jit(solution)/shard_map/ppermute | solution.py:12
  213.7 3.6 %collective-permute-start.1 = (bf16[4,1,32,16]{3,2,1,0:T(8,128)(2,1)S(1)}, bf16[4,1,32,16]{3,2,1,0:T(8,128)(2,1)S(1)}, u32[]{:S(2)}, u32[]{:S(2)}) collective-permute-start(bf16[4,1,32,16]{3,2,1,0:T(8,128)(2,1)S(1)} %get-tuple-element.63), channel_id=1, source_target_pairs={{0,4},{4,8},{8,12},{1,5},{5,9},{9,13},{2,6},{6,10},{10,14},{3,7},{... | collective-permute-start | bytes 12296 | tf_op jit(solution)/shard_map/ppermute | solution.py:22
  217.3 1.3 collective-permute-start.2
  218.6 0.3 collective-permute-done.1
  218.9 4.2 %collective-permute-done.2 = bf16[4,1,32,16]{3,2,1,0:T(8,128)(2,1)S(1)} collective-permute-done((bf16[4,1,32,16]{3,2,1,0:T(8,128)(2,1)S(1)}, bf16[4,1,32,16]{3,2,1,0:T(8,128)(2,1)S(1)}, u32[]{:S(2)}, u32[]{:S(2)}) %collective-permute-start.2) | collective-permute-done | bytes 4128 | tf_op jit(solution)/shard_map/ppermute | solution.py:23
  223.1 0.1 select_maximum_fusion
  223.2 0.0 copy-start.3
  223.2 0.0 copy-start.11
  223.2 0.0 copy-start.12
  223.2 0.1 fusion.32
  223.4 0.3 concatenate.105
  223.7 0.4 copy-done.3
  224.2 0.3 multiply_reduce_fusion
  224.5 0.8 multiply_convert_fusion
  (31 shorter events, 0.2 us)
Async XLA Ops:
  7.2 200.8 %copy-start = (bf16[5120,64]{0,1:T(8,128)(2,1)S(1)}, bf16[5120,64]{0,1:T(8,128)(2,1)}, u32[]{:S(2)}) copy-start(bf16[5120,64]{0,1:T(8,128)(2,1)} %param.21) | copy-start | bytes 1966084
  7.2 1.0 copy-start.5
  7.2 169.8 %all-gather.2.cloned.1.call-start = ((), (), s32[]{:S(2)}) async-start(), calls=%async_computation.4 | async-start | bytes 9830400 | tf_op jit(solution)/shard_map/all_gather | solution.py:160
  8.2 7.4 %copy-start.6 = (bf16[2,1,16,3072]{3,2,1,0:T(8,128)(2,1)S(1)}, bf16[2,1,16,3072]{3,2,1,0:T(8,128)(2,1)}, u32[]{:S(2)}) copy-start(bf16[2,1,16,3072]{3,2,1,0:T(8,128)(2,1)} %param.13) | copy-start | bytes 589828
  12.3 7.5 %all-to-all-start.1 = ((bf16[4,2,12288]{2,1,0:T(2,128)(2,1)}), bf16[4,2,12288]{2,1,0:T(2,128)(2,1)S(1)}, u32[]{:S(2)}, u32[]{:S(2)}) async-start(bf16[4,2,12288]{2,1,0:T(2,128)(2,1)} %reshape.122), calls=%async_computation.1 | async-start | bytes 393216 | tf_op jit(solution)/shard_map/all_to_all | solution.py:132
  17.5 6.7 %copy-start.7 = (bf16[2,1,16,3072]{3,2,1,0:T(8,128)(2,1)S(1)}, bf16[2,1,16,3072]{3,2,1,0:T(8,128)(2,1)}, u32[]{:S(2)}) copy-start(bf16[2,1,16,3072]{3,2,1,0:T(8,128)(2,1)} %param.15) | copy-start | bytes 589828
  19.8 10.8 %all-to-all-start = ((bf16[4,2,12288]{2,1,0:T(2,128)(2,1)}), bf16[4,2,12288]{2,1,0:T(2,128)(2,1)S(1)}, u32[]{:S(2)}, u32[]{:S(2)}) async-start(bf16[4,2,12288]{2,1,0:T(2,128)(2,1)} %reshape.124), calls=%async_computation | async-start | bytes 393216 | tf_op jit(solution)/shard_map/all_to_all | solution.py:131
  30.6 42.8 %all-to-all-start.2 = ((bf16[4,2,12288]{2,1,0:T(2,128)(2,1)}), bf16[4,2,12288]{2,1,0:T(2,128)(2,1)}, u32[]{:S(2)}, u32[]{:S(2)}) async-start(bf16[4,2,12288]{2,1,0:T(2,128)(2,1)} %reshape.126), calls=%async_computation.2 | async-start | bytes 393216 | tf_op jit(solution)/shard_map/all_to_all | solution.py:133
  34.6 171.7 %reduce-scatter.2.cloned.1.call-start = ((), (), s32[]{:S(2)}) async-start(), calls=%async_computation.5 | async-start | bytes 1638400 | tf_op jit(solution)/shard_map/reduce_scatter | solution.py:164
  116.8 1.2 copy-start.2
  119.1 63.5 %copy-start.9 = (f32[5120]{0:T(1024)S(1)}, f32[5120]{0:T(1024)}, u32[]{:S(2)}) copy-start(f32[5120]{0:T(1024)} %param.20) | copy-start | bytes 61444
  119.1 87.2 %copy-start.10 = (f32[5120]{0:T(1024)S(1)}, f32[5120]{0:T(1024)}, u32[]{:S(2)}) copy-start(f32[5120]{0:T(1024)} %param.18) | copy-start | bytes 61444
  182.6 23.8 %copy-start.4 = (bf16[2,1,16,5120]{3,2,1,0:T(8,128)(2,1)S(1)}, bf16[2,1,16,5120]{3,2,1,0:T(8,128)(2,1)}, u32[]{:S(2)}) copy-start(bf16[2,1,16,5120]{3,2,1,0:T(8,128)(2,1)} %param.16) | copy-start | bytes 983044
  182.6 25.2 %copy-start.8 = (f32[5120]{0:T(1024)S(1)}, f32[5120]{0:T(1024)}, u32[]{:S(2)}) copy-start(f32[5120]{0:T(1024)} %param.19) | copy-start | bytes 61444
  182.6 25.4 %copy-start.13 = (f32[64]{0:T(128)S(1)}, f32[64]{0:T(128)}, u32[]{:S(2)}) copy-start(f32[64]{0:T(128)} %param.22) | copy-start | bytes 772
  207.5 15.8 %copy-start.1 = (bf16[2,1,16,5120]{3,2,0,1:T(8,128)(2,1)}, bf16[2,1,16,5120]{3,2,0,1:T(8,128)(2,1)S(1)}, u32[]{:S(2)}) copy-start(bf16[2,1,16,5120]{3,2,0,1:T(8,128)(2,1)S(1)} %get-tuple-element.36) | copy-start | bytes 983044
  208.4 5.2 %collective-permute-start = (bf16[2,2,32,16]{3,2,1,0:T(8,128)(2,1)S(1)}, bf16[2,2,32,16]{3,2,1,0:T(8,128)(2,1)S(1)}, u32[]{:S(2)}, u32[]{:S(2)}) collective-permute-start(bf16[2,2,32,16]{3,2,1,0:T(8,128)(2,1)S(1)} %bitcast.101), channel_id=1, source_target_pairs={{0,1},{1,2},{2,3},{4,5},{5,6},{6,7},{8,9},{9,10},{10,11},{12,13},{... | collective-permute-start | bytes 12296 | tf_op jit(solution)/shard_map/ppermute | solution.py:12
  213.7 5.2 %collective-permute-start.1 = (bf16[4,1,32,16]{3,2,1,0:T(8,128)(2,1)S(1)}, bf16[4,1,32,16]{3,2,1,0:T(8,128)(2,1)S(1)}, u32[]{:S(2)}, u32[]{:S(2)}) collective-permute-start(bf16[4,1,32,16]{3,2,1,0:T(8,128)(2,1)S(1)} %get-tuple-element.63), channel_id=1, source_target_pairs={{0,4},{4,8},{8,12},{1,5},{5,9},{9,13},{2,6},{6,10},{10,14},{3,7},{... | collective-permute-start | bytes 12296 | tf_op jit(solution)/shard_map/ppermute | solution.py:22
  217.3 5.8 %collective-permute-start.2 = (bf16[4,1,32,16]{3,2,1,0:T(8,128)(2,1)S(1)}, bf16[4,1,32,16]{3,2,1,0:T(8,128)(2,1)S(1)}, u32[]{:S(2)}, u32[]{:S(2)}) collective-permute-start(bf16[4,1,32,16]{3,2,1,0:T(8,128)(2,1)S(1)} %get-tuple-element.64), channel_id=1, source_target_pairs={{4,0},{8,4},{12,8},{5,1},{9,5},{13,9},{6,2},{10,6},{14,10},{7,3},{... | collective-permute-start | bytes 12296 | tf_op jit(solution)/shard_map/ppermute | solution.py:23
  223.2 1.0 copy-start.3
  223.2 1.0 copy-start.11
  223.2 1.3 copy-start.12
Sparse Core Ops, SparseCore 0:
  9.6 167.3 all-gather.1
  182.7 23.5 reduce-scatter.1
where the time goes:
time: 233 us; the launch traced here: 232 us
  waiting for transfers between devices  90.1 us (39%)
  blocking collectives  67.6 us (29%)
  local copies, waits for them, and re-layouts  30.9 us (13%)
  starting transfers between devices  18.7 us (8%)
  between operations  14.4 us (6%)
  matrix products  7.28 us (3%)
  other arithmetic  3.08 us (1%)
    all_gather x1, waiting for transfers between devices, on_device(): lax.all_gather(out_weight, 'seq', axis=1, tiled=True)  57.9 us
    all_gather x1, blocking collectives, on_device(): lax.all_gather(local_keys, 'seq', axis=1, tiled=True)  35.2 us
    all_gather x1, blocking collectives, on_device(): lax.all_gather(local_values, 'seq', axis=1, tiled=True)  32.4 us
    reduce_scatter x1, waiting for transfers between devices, on_device(): lax.psum_scatter(partial_value.astype(jnp.bfloat16), 'head', scatter_dime...  23.7 us
    unnamed x37, local copies, waits for them, and re-layouts  21.1 us
    dot_general x1, matrix products, on_device(): jnp.dot(attended, lax.all_gather(out_weight, 'seq', axis=1, tiled=True),...  5.58 us
  transfers between devices with their start and end apart: 8, of which 5 were waited for; matrix products, arithmetic and copies ran while one was open for 13% of the time, Pallas kernels for 0%

commit v1 on v0

--- a/solution.py
+++ b/solution.py
@@ -155,10 +155,11 @@
     running, denominator, weighted = carried
     attended = (weighted / denominator[..., None]).astype(jnp.bfloat16)
     attended = attended.transpose(1, 0, 2).reshape(count, group_width)
+    turn_node = lambda body, device_axis, axis_no: jnp.concatenate(
+        lax.all_gather(body, axis_name=device_axis), axis=axis_no
+    )
     partial_value = jnp.dot(
-        attended,
-        lax.all_gather(out_weight, "seq", axis=1, tiled=True),
-        preferred_element_type=jnp.float32,
+        attended, turn_node(out_weight, "seq", 1), preferred_element_type=jnp.float32
     )
     partial_value = partial_value.reshape(frames_all, height, breadth, partial_value.shape[-1])
     owned = lax.psum_scatter(

time: 233 us -> 259 us (1.11)
  local copies, waits for them, and re-layouts: 30.9 us -> 57.3 us
    reshape x0 -> x1, local copies, waits for them, and re-layouts: none -> 13.9 us  [on_device(): jnp.concatenate(lax.all_gather(body, axis_name=device_axis), axis=axis_no)]
    all_gather x0 -> x1, local copies, waits for them, and re-layouts: none -> 12.4 us  [on_device(): lax.all_gather(body, axis_name=device_axis)]
  transfers between devices with their start and end apart: 8 -> 8, of which waited for: 5 -> 5; matrix products, arithmetic and copies ran while one was open for 13% -> 12% of each run, Pallas kernels for 0% -> 0%
where the time goes in v1:
time: 259 us; the launch traced here: 258 us
  waiting for transfers between devices  90.1 us (35%)
  blocking collectives  67.6 us (26%)
  local copies, waits for them, and re-layouts  57.3 us (22%)
  starting transfers between devices  18.7 us (7%)
  between operations  14.4 us (6%)
  matrix products  7.29 us (3%)
  other arithmetic  3.07 us (1%)
    all_gather x1, waiting for transfers between devices, on_device(): lax.all_gather(body, axis_name=device_axis)  58 us
    all_gather x1, blocking collectives, on_device(): lax.all_gather(local_keys, 'seq', axis=1, tiled=True)  35.2 us
    all_gather x1, blocking collectives, on_device(): lax.all_gather(local_values, 'seq', axis=1, tiled=True)  32.3 us
    reduce_scatter x1, waiting for transfers between devices, on_device(): lax.psum_scatter(partial_value.astype(jnp.bfloat16), 'head', scatter_dime...  23.7 us
    unnamed x37, local copies, waits for them, and re-layouts  21.1 us
    reshape x1, local copies, waits for them, and re-layouts, on_device(): jnp.concatenate(lax.all_gather(body, axis_name=device_axis), axis=axis_no)  13.9 us
    all_gather x1, local copies, waits for them, and re-layouts, on_device(): lax.all_gather(body, axis_name=device_axis)  12.4 us
    dot_general x1, matrix products, on_device(): jnp.dot(attended, turn_node(out_weight, 'seq', 1), preferred_element_type...  5.59 us
  transfers between devices with their start and end apart: 8, of which 5 were waited for; matrix products, arithmetic and copies ran while one was open for 12% of the time, Pallas kernels for 0%

profile of v1, /device:TPU:2, one launch (start us, length us, event | category | flops | bytes accessed | tf_op | source)
XLA Modules:
  0.0 258.5 jit_solution(16982671155406756970)
XLA Ops:
  7.2 0.0 copy-start
  7.2 0.0 all-gather.3.cloned.1.call-start
  7.2 0.7 all-gather.3.cloned.1.call-update
  7.9 0.2 copy-done.5
  8.2 1.8 copy.84
  10.0 2.3 reshape.132
  12.3 3.4 %all-to-all-start.1 = ((bf16[4,2,12288]{2,1,0:T(2,128)(2,1)}), bf16[4,2,12288]{2,1,0:T(2,128)(2,1)S(1)}, u32[]{:S(2)}, u32[]{:S(2)}) async-start(bf16[4,2,12288]{2,1,0:T(2,128)(2,1)} %reshape.132), calls=%async_computation.1 | async-start | bytes 393216 | tf_op jit(solution)/shard_map/all_to_all | solution.py:132
  15.6 0.0 copy-start.7
  15.6 1.8 copy.80
  17.5 2.3 reshape.134
  19.8 4.4 %all-to-all-start = ((bf16[4,2,12288]{2,1,0:T(2,128)(2,1)}), bf16[4,2,12288]{2,1,0:T(2,128)(2,1)S(1)}, u32[]{:S(2)}, u32[]{:S(2)}) async-start(bf16[4,2,12288]{2,1,0:T(2,128)(2,1)} %reshape.134), calls=%async_computation | async-start | bytes 393216 | tf_op jit(solution)/shard_map/all_to_all | solution.py:131
  24.2 1.8 copy.89
  26.0 2.3 reshape.136
  28.3 1.2 reshape.133
  29.4 1.1 copy.99
  30.6 0.0 all-to-all-done
  30.6 4.0 %all-to-all-start.2 = ((bf16[4,2,12288]{2,1,0:T(2,128)(2,1)}), bf16[4,2,12288]{2,1,0:T(2,128)(2,1)}, u32[]{:S(2)}, u32[]{:S(2)}) async-start(bf16[4,2,12288]{2,1,0:T(2,128)(2,1)} %reshape.136), calls=%async_computation.2 | async-start | bytes 393216 | tf_op jit(solution)/shard_map/all_to_all | solution.py:133
  34.6 0.0 reduce-scatter.2.cloned.1.call-start
  34.7 35.2 %all_gather.12 = bf16[8,4,16,768]{3,2,0,1:T(8,128)(2,1)S(1)} all-gather(bf16[8,1,16,768]{3,2,0,1:T(8,128)(2,1)S(1)} %bitcast.111), channel_id=1, replica_groups=mesh['clip'=2,'seq'=4,'head'=4] {'seq'}, dimensions={1}, use_global_device_ids=true | all-gather | bytes 983040 | tf_op jit(solution)/shard_map/all_gather | solution.py:151
  69.9 1.2 reshape.135
  71.1 1.1 copy.98
  72.2 0.2 reshape.121
  72.4 0.1 copy.87
  72.5 0.9 squeeze.9
  73.4 0.0 all-to-all-done.2
  73.4 5.6 %reshape.137 = bf16[3072,1,2,16]{3,2,1,0:T(2,128)(2,1)S(1)} reshape(bf16[4,2,12288]{2,1,0:T(2,128)(2,1)} %all-to-all-done.2) | data formatting | bytes 393216
  79.0 2.5 copy.100
  81.5 1.0 copy.91
  82.4 32.3 %all_gather.13 = bf16[8,4,16,768]{3,2,0,1:T(8,128)(2,1)S(1)} all-gather(bf16[8,1,16,768]{3,2,0,1:T(8,128)(2,1)S(1)} %bitcast.112), channel_id=1, replica_groups=mesh['clip'=2,'seq'=4,'head'=4] {'seq'}, dimensions={1}, use_global_device_ids=true | all-gather | bytes 983040 | tf_op jit(solution)/shard_map/all_gather | solution.py:152
  114.8 0.1 copy.92
  114.9 1.9 squeeze.10
  116.8 0.5 fusion.28
  117.2 0.5 fusion.1
  117.8 0.2 copy-done.2
  118.0 0.6 fusion.5
  118.6 0.1 copy.94
  118.8 0.2 dot_general.24
  119.0 58.0 %all-gather.3.cloned.1.call-done = bf16[3072,1280]{1,0:T(8,128)(2,1)} async-done(((bf16[768,1280]{1,0:T(8,128)(2,1)}), bf16[3072,1280]{1,0:T(8,128)(2,1)}) %all-gather.3.cloned.1.call-update) | async-done | bytes 7864336 | tf_op jit(solution)/shard_map/all_gather | solution.py:159
  177.0 12.4 %copy.114 = bf16[4,768,1280]{2,0,1:T(4,128)(2,1)} copy(bf16[4,768,1280]{2,1,0:T(8,128)(2,1)} %bitcast.92) | data formatting | bytes 15728640 | tf_op jit(solution)/shard_map/all_gather | solution.py:159
  189.4 13.9 %reshape.130 = bf16[768,5120,1]{1,0,2:T(8,128)(2,1)} reshape(bf16[768,4,1280]{2,1,0:T(4,128)(2,1)} %bitcast.91) | data formatting | bytes 15728640 | tf_op jit(solution)/shard_map/reshape | solution.py:158
  203.4 5.6 %fusion = bf16[8,1,16,5120]{3,2,0,1:T(8,128)(2,1)} fusion(bf16[8,16,768]{2,1,0:T(8,128)(2,1)S(1)} %dot_general.24, bf16[768,5120,1]{1,0,2:T(8,128)(2,1)} %reshape.130), kind=kOutput, calls=%fused_computation.2 | convolution fusion | flops 1007288320 | bytes 9371648 | tf_op jit(solution)/shard_map/dot_general | solution.py:161
  209.0 0.0 reduce-scatter.2.cloned.1.call-update
  209.0 23.7 %reduce-scatter.2.cloned.1.call-done = bf16[2,1,16,5120]{3,2,0,1:T(8,128)(2,1)} async-done(((bf16[8,1,16,5120]{3,2,0,1:T(8,128)(2,1)}), bf16[2,1,16,5120]{3,2,0,1:T(8,128)(2,1)}) %reduce-scatter.2.cloned.1.call-update) | async-done | bytes 327696 | tf_op jit(solution)/shard_map/reduce_scatter | solution.py:165
  232.7 1.2 convert_reduce_fusion
  233.9 0.2 fusion.13
  234.1 0.0 copy-done.8
  234.1 0.2 fusion.16
  234.4 0.3 fusion.6
  234.7 0.1 reshape.125
  234.8 1.9 collective-permute-start
  236.7 3.3 %collective-permute-done = bf16[2,2,32,16]{3,2,1,0:T(8,128)(2,1)S(1)} collective-permute-done((bf16[2,2,32,16]{3,2,1,0:T(8,128)(2,1)S(1)}, bf16[2,2,32,16]{3,2,1,0:T(8,128)(2,1)S(1)}, u32[]{:S(2)}, u32[]{:S(2)}) %collective-permute-start) | collective-permute-done | bytes 4128 | tf_op jit(solution)/shard_map/ppermute | solution.py:12
  240.0 3.6 %collective-permute-start.1 = (bf16[4,1,32,16]{3,2,1,0:T(8,128)(2,1)S(1)}, bf16[4,1,32,16]{3,2,1,0:T(8,128)(2,1)S(1)}, u32[]{:S(2)}, u32[]{:S(2)}) collective-permute-start(bf16[4,1,32,16]{3,2,1,0:T(8,128)(2,1)S(1)} %get-tuple-element.63), channel_id=1, source_target_pairs={{0,4},{4,8},{8,12},{1,5},{5,9},{9,13},{2,6},{6,10},{10,14},{3,7},{... | collective-permute-start | bytes 12296 | tf_op jit(solution)/shard_map/ppermute | solution.py:22
  243.7 1.3 collective-permute-start.2
  245.0 0.3 collective-permute-done.1
  245.3 4.2 %collective-permute-done.2 = bf16[4,1,32,16]{3,2,1,0:T(8,128)(2,1)S(1)} collective-permute-done((bf16[4,1,32,16]{3,2,1,0:T(8,128)(2,1)S(1)}, bf16[4,1,32,16]{3,2,1,0:T(8,128)(2,1)S(1)}, u32[]{:S(2)}, u32[]{:S(2)}) %collective-permute-start.2) | collective-permute-done | bytes 4128 | tf_op jit(solution)/shard_map/ppermute | solution.py:23
  249.5 0.1 select_maximum_fusion
  249.6 0.0 copy-start.3
  249.6 0.0 copy-start.11
  249.6 0.0 copy-start.12
  249.6 0.1 fusion.25
  249.8 0.3 concatenate.105
  250.1 0.4 copy-done.3
  250.5 0.3 multiply_reduce_fusion
  250.9 0.8 multiply_convert_fusion
  (33 shorter events, 0.2 us)
Async XLA Ops:
  7.2 227.2 %copy-start = (bf16[5120,64]{0,1:T(8,128)(2,1)S(1)}, bf16[5120,64]{0,1:T(8,128)(2,1)}, u32[]{:S(2)}) copy-start(bf16[5120,64]{0,1:T(8,128)(2,1)} %param.21) | copy-start | bytes 1966084
  7.2 1.0 copy-start.5
  7.2 169.8 %all-gather.3.cloned.1.call-start = ((), (), s32[]{:S(2)}) async-start(), calls=%async_computation.5 | async-start | bytes 9830400 | tf_op jit(solution)/shard_map/all_gather | solution.py:159
  8.2 7.4 %copy-start.6 = (bf16[2,1,16,3072]{3,2,1,0:T(8,128)(2,1)S(1)}, bf16[2,1,16,3072]{3,2,1,0:T(8,128)(2,1)}, u32[]{:S(2)}) copy-start(bf16[2,1,16,3072]{3,2,1,0:T(8,128)(2,1)} %param.13) | copy-start | bytes 589828
  12.3 7.5 %all-to-all-start.1 = ((bf16[4,2,12288]{2,1,0:T(2,128)(2,1)}), bf16[4,2,12288]{2,1,0:T(2,128)(2,1)S(1)}, u32[]{:S(2)}, u32[]{:S(2)}) async-start(bf16[4,2,12288]{2,1,0:T(2,128)(2,1)} %reshape.132), calls=%async_computation.1 | async-start | bytes 393216 | tf_op jit(solution)/shard_map/all_to_all | solution.py:132
  15.6 8.6 %copy-start.7 = (bf16[2,1,16,3072]{3,2,1,0:T(8,128)(2,1)S(1)}, bf16[2,1,16,3072]{3,2,1,0:T(8,128)(2,1)}, u32[]{:S(2)}) copy-start(bf16[2,1,16,3072]{3,2,1,0:T(8,128)(2,1)} %param.15) | copy-start | bytes 589828
  19.8 10.8 %all-to-all-start = ((bf16[4,2,12288]{2,1,0:T(2,128)(2,1)}), bf16[4,2,12288]{2,1,0:T(2,128)(2,1)S(1)}, u32[]{:S(2)}, u32[]{:S(2)}) async-start(bf16[4,2,12288]{2,1,0:T(2,128)(2,1)} %reshape.134), calls=%async_computation | async-start | bytes 393216 | tf_op jit(solution)/shard_map/all_to_all | solution.py:131
  30.6 42.8 %all-to-all-start.2 = ((bf16[4,2,12288]{2,1,0:T(2,128)(2,1)}), bf16[4,2,12288]{2,1,0:T(2,128)(2,1)}, u32[]{:S(2)}, u32[]{:S(2)}) async-start(bf16[4,2,12288]{2,1,0:T(2,128)(2,1)} %reshape.136), calls=%async_computation.2 | async-start | bytes 393216 | tf_op jit(solution)/shard_map/all_to_all | solution.py:133
  34.6 198.1 %reduce-scatter.2.cloned.1.call-start = ((), (), s32[]{:S(2)}) async-start(), calls=%async_computation.4 | async-start | bytes 1638400 | tf_op jit(solution)/shard_map/reduce_scatter | solution.py:165
  116.8 1.2 copy-start.2
  203.4 5.6 %copy-start.9 = (f32[5120]{0:T(1024)S(1)}, f32[5120]{0:T(1024)}, u32[]{:S(2)}) copy-start(f32[5120]{0:T(1024)} %param.20) | copy-start | bytes 61444
  203.4 29.3 %copy-start.10 = (f32[5120]{0:T(1024)S(1)}, f32[5120]{0:T(1024)}, u32[]{:S(2)}) copy-start(f32[5120]{0:T(1024)} %param.18) | copy-start | bytes 61444
  209.0 23.7 %copy-start.4 = (bf16[2,1,16,5120]{3,2,1,0:T(8,128)(2,1)S(1)}, bf16[2,1,16,5120]{3,2,1,0:T(8,128)(2,1)}, u32[]{:S(2)}) copy-start(bf16[2,1,16,5120]{3,2,1,0:T(8,128)(2,1)} %param.16) | copy-start | bytes 983044
  209.0 25.2 %copy-start.8 = (f32[5120]{0:T(1024)S(1)}, f32[5120]{0:T(1024)}, u32[]{:S(2)}) copy-start(f32[5120]{0:T(1024)} %param.19) | copy-start | bytes 61444
  209.0 25.4 %copy-start.13 = (f32[64]{0:T(128)S(1)}, f32[64]{0:T(128)}, u32[]{:S(2)}) copy-start(f32[64]{0:T(128)} %param.22) | copy-start | bytes 772
  233.9 15.8 %copy-start.1 = (bf16[2,1,16,5120]{3,2,0,1:T(8,128)(2,1)}, bf16[2,1,16,5120]{3,2,0,1:T(8,128)(2,1)S(1)}, u32[]{:S(2)}) copy-start(bf16[2,1,16,5120]{3,2,0,1:T(8,128)(2,1)S(1)} %get-tuple-element.36) | copy-start | bytes 983044
  234.8 5.2 %collective-permute-start = (bf16[2,2,32,16]{3,2,1,0:T(8,128)(2,1)S(1)}, bf16[2,2,32,16]{3,2,1,0:T(8,128)(2,1)S(1)}, u32[]{:S(2)}, u32[]{:S(2)}) collective-permute-start(bf16[2,2,32,16]{3,2,1,0:T(8,128)(2,1)S(1)} %bitcast.101), channel_id=1, source_target_pairs={{0,1},{1,2},{2,3},{4,5},{5,6},{6,7},{8,9},{9,10},{10,11},{12,13},{... | collective-permute-start | bytes 12296 | tf_op jit(solution)/shard_map/ppermute | solution.py:12
  240.0 5.2 %collective-permute-start.1 = (bf16[4,1,32,16]{3,2,1,0:T(8,128)(2,1)S(1)}, bf16[4,1,32,16]{3,2,1,0:T(8,128)(2,1)S(1)}, u32[]{:S(2)}, u32[]{:S(2)}) collective-permute-start(bf16[4,1,32,16]{3,2,1,0:T(8,128)(2,1)S(1)} %get-tuple-element.63), channel_id=1, source_target_pairs={{0,4},{4,8},{8,12},{1,5},{5,9},{9,13},{2,6},{6,10},{10,14},{3,7},{... | collective-permute-start | bytes 12296 | tf_op jit(solution)/shard_map/ppermute | solution.py:22
  243.7 5.8 %collective-permute-start.2 = (bf16[4,1,32,16]{3,2,1,0:T(8,128)(2,1)S(1)}, bf16[4,1,32,16]{3,2,1,0:T(8,128)(2,1)S(1)}, u32[]{:S(2)}, u32[]{:S(2)}) collective-permute-start(bf16[4,1,32,16]{3,2,1,0:T(8,128)(2,1)S(1)} %get-tuple-element.64), channel_id=1, source_target_pairs={{4,0},{8,4},{12,8},{5,1},{9,5},{13,9},{6,2},{10,6},{14,10},{7,3},{... | collective-permute-start | bytes 12296 | tf_op jit(solution)/shard_map/ppermute | solution.py:23
  249.6 1.0 copy-start.3
  249.6 1.0 copy-start.11
  249.6 1.3 copy-start.12
Sparse Core Ops, SparseCore 0:
  9.6 167.3 all-gather.2
  209.1 23.5 reduce-scatter.1
